TPU v7x, 32 devices: a whole 2x2x4 slice. The times are simulated.
32 devices in a mesh: expert: 8 (over y, x, core), tensor: 4 (over z).
Axes of the slice: x: 2, y: 2, z: 4, core: 2. Of those that a mesh axis runs over, the one named last changes fastest.
Arguments:
- tokens: bfloat16 [1024, 2560], P('expert', 'tensor'), may hold values from -6 to 6
- slot: int32 [1024, 1], P('expert'), may hold values from 0 to 15; in each aligned block of 128 rows (0 to 127, 128 to 255, ...) at most 16 rows name the same one
- mask: int32 [1024], P('expert'), may hold values 0 or 1
- hot_group: int32 [1], replicated, may hold values from 0 to 7
- router_weight: bfloat16 [2560, 8], replicated, may hold values from -0.125 to 0.125
- exp_gate: bfloat16 [8, 2560, 4096], P('expert', None, 'tensor'), may hold values from -0.125 to 0.125
- exp_up: bfloat16 [8, 2560, 4096], P('expert', None, 'tensor'), may hold values from -0.125 to 0.125
- exp_down: bfloat16 [8, 4096, 2560], P('expert', 'tensor'), may hold values from -0.09375 to 0.09375
- sh_gate: bfloat16 [2560, 4096], P('expert', 'tensor'), may hold values from -0.125 to 0.125
- sh_up: bfloat16 [2560, 4096], P('expert', 'tensor'), may hold values from -0.125 to 0.125
- sh_down: bfloat16 [4096, 2560], P('tensor', 'expert'), may hold values from -0.09375 to 0.09375
Outputs:
- mixed: bfloat16 [1024, 2560], P('expert', 'tensor')
Inputs may be any that keep to these rules, and one draw needn't show every extreme that they name: Slot 2 g is the home slot of expert g, slot 2 g + 1 the spare slot of group g. Among the 128 tokens of one group no slot is named by more than 16 tokens, a bound that some block reaches.
All inputs are finite; a program needn't handle non-finite values. No bound on the sum of `mask` on one device may be relied on, other than what follows from the above.
Results may differ from a plain program's by a relative error of at most 0.0052.
Values may be sent and summed in bfloat16 or wider, within the bound.
No kernel may reach another device: no remote copies, remote signals or barrier semaphores. Data moves between devices by JAX's collectives and lax.ppermute only.
A program may use at most 192 MiB of HBM per device.

v0:
```python
import jax
import jax.numpy as jnp
from jax import lax
from jax.sharding import PartitionSpec as P


def from_root(block, axis, source):
    block = jnp.where(lax.axis_index(axis) == source, block, jnp.zeros_like(block))
    return lax.psum(block, axis)


def expert_ffn(batch_rows, w_gate, w_up, w_down):
    gated = jnp.dot(batch_rows, w_gate, preferred_element_type=jnp.float32)
    upward = jnp.dot(batch_rows, w_up, preferred_element_type=jnp.float32)
    hidden = (jax.nn.silu(gated) * upward).astype(jnp.bfloat16)
    return jnp.dot(hidden, w_down, preferred_element_type=jnp.float32)


def local(
    tokens,
    slot,
    mask,
    hot_group,
    router_weight,
    exp_gate,
    exp_up,
    exp_down,
    sh_gate,
    sh_up,
    sh_down,
):
    n_groups = lax.axis_size("expert")
    whole = lax.all_gather(tokens, "tensor", axis=1, tiled=True)
    tok_count = whole.shape[0]
    width = whole.shape[1]
    capacity = tok_count // n_groups
    slot_count = 2 * n_groups
    slot_ids = slot[:, 0]
    hot_index = hot_group[0]
    expert_id = jnp.where(slot_ids % 2 == 0, slot_ids // 2, hot_index)
    logits = jnp.dot(whole, router_weight, preferred_element_type=jnp.float32)
    chosen = expert_id[:, None] == lax.broadcasted_iota(jnp.int32, (1, router_weight.shape[1]), 1)
    weighting = jax.nn.sigmoid(jnp.sum(jnp.where(chosen, logits, 0.0), axis=1))
    shared_gate = jnp.dot(
        whole,
        lax.all_gather(sh_gate, "expert", axis=0, tiled=True),
        preferred_element_type=jnp.float32,
    )
    shared_up = jnp.dot(
        whole,
        lax.all_gather(sh_up, "expert", axis=0, tiled=True),
        preferred_element_type=jnp.float32,
    )
    sh_hidden = (jax.nn.silu(shared_gate) * shared_up).astype(jnp.bfloat16)
    shared_terms = jnp.dot(
        sh_hidden,
        lax.all_gather(sh_down, "expert", axis=1, tiled=True),
        preferred_element_type=jnp.float32,
    )
    shared = lax.psum_scatter(shared_terms, "tensor", scatter_dimension=1, tiled=True)
    slot_hits = (slot_ids[:, None] == lax.broadcasted_iota(jnp.int32, (1, slot_count), 1)).astype(
        jnp.int32
    )
    position = jnp.sum((jnp.cumsum(slot_hits, axis=0) - 1) * slot_hits, axis=1)
    target = slot_ids * capacity + position
    placing = (
        lax.broadcasted_iota(jnp.int32, (slot_count * capacity, 1), 0) == target[None, :]
    ).astype(jnp.bfloat16)
    outgoing = jnp.dot(placing, tokens, preferred_element_type=jnp.float32).astype(jnp.bfloat16)
    quarter = lax.all_to_all(outgoing, "expert", split_axis=0, concat_axis=0, tiled=True)
    arrived = lax.all_gather(quarter, "tensor", axis=1, tiled=True)
    replica = (
        from_root(exp_gate[0], "expert", hot_index),
        from_root(exp_up[0], "expert", hot_index),
        from_root(exp_down[0], "expert", hot_index),
    )
    grouped = arrived.reshape(n_groups, 2, capacity, width)
    home_rows = grouped[:, 0].reshape(n_groups * capacity, width)
    spare_rows = grouped[:, 1].reshape(n_groups * capacity, width)
    home_part = expert_ffn(home_rows, exp_gate[0], exp_up[0], exp_down[0])
    spare_part = expert_ffn(spare_rows, replica[0], replica[1], replica[2])
    partials = jnp.stack(
        [
            home_part.reshape(n_groups, capacity, width),
            spare_part.reshape(n_groups, capacity, width),
        ],
        axis=1,
    )
    partials = partials.reshape(slot_count * capacity, width)
    summed = lax.psum_scatter(partials, "tensor", scatter_dimension=1, tiled=True).astype(
        jnp.bfloat16
    )
    returned = lax.all_to_all(summed, "expert", split_axis=0, concat_axis=0, tiled=True)
    routed = lax.dot_general(
        placing, returned, (((0,), (0,)), ((), ())), preferred_element_type=jnp.float32
    )
    keep_rows = mask.astype(jnp.float32)
    mixed = keep_rows[:, None] * (shared + weighting[:, None] * routed)
    return mixed.astype(jnp.bfloat16)


def solution(mesh):
    in_specs = (
        P("expert", "tensor"),
        P("expert", None),
        P("expert"),
        P(),
        P(),
        P("expert", None, "tensor"),
        P("expert", None, "tensor"),
        P("expert", "tensor", None),
        P("expert", "tensor"),
        P("expert", "tensor"),
        P("tensor", "expert"),
    )
    out_specs = P("expert", "tensor")
    return jax.shard_map(local, mesh=mesh, in_specs=in_specs, out_specs=out_specs, check_vma=False)
```

profile of v0, /device:TPU:0, one launch (start us, length us, event | category | flops | bytes accessed | tf_op | source)
XLA Modules:
  0.0 397.9 jit_solution(10795923195216460951)
XLA Ops:
  7.4 0.7 fusion.37
  8.1 0.2 reduce_window_sum.11
  8.3 0.8 select_reduce_fusion
  9.1 0.7 multiply_add_fusion
  9.8 1.9 convolution_convert_fusion
  11.7 5.2 %all-to-all-start = ((bf16[8,32,640]{2,1,0:T(8,128)(2,1)}), bf16[8,32,640]{2,1,0:T(8,128)(2,1)S(1)}, u32[]{:S(2)}, u32[]{:S(2)}) async-start(bf16[8,32,640]{2,1,0:T(8,128)(2,1)} %bitcast.3), calls=%async_computation.1 | async-start | bytes 655360 | tf_op jit(solution)/shard_map/all_to_all | solution.py:70
  17.6 6.9 %all-to-all-done = bf16[8,32,640]{2,1,0:T(8,128)(2,1)S(1)} async-done(((bf16[8,32,640]{2,1,0:T(8,128)(2,1)}), bf16[8,32,640]{2,1,0:T(8,128)(2,1)S(1)}, u32[]{:S(2)}, u32[]{:S(2)}) %all-to-all-start) | async-done | bytes 327712 | tf_op jit(solution)/shard_map/all_to_all | solution.py:70
  24.5 0.7 copy-done.1
  25.3 5.1 %bitcast_select_fusion = bf16[1024,2560]{1,0:T(8,128)(2,1)} fusion(bf16[1,1024,2560]{2,1,0:T(8,128)(2,1)} %param.18, pred[]{:T(512)S(6)} %eq.64), kind=kLoop, calls=%fused_computation.2 | loop fusion | flops 2621440 | bytes 10485761 | tf_op jit(solution)/shard_map/jit(_where)/select_n | solution.py:8
  30.4 9.0 %bitcast_select_fusion.1 = (bf16[2560,1024]{1,0:T(8,128)(2,1)}, bf16[2560,1024]{1,0:T(8,128)(2,1)}) fusion(bf16[1,2560,1024]{2,1,0:T(8,128)(2,1)} %param.17, pred[]{:T(512)S(6)} %eq.64, bf16[1,2560,1024]{2,1,0:T(8,128)(2,1)} %param.16), kind=kLoop, calls=%fused_computation.3 | loop fusion | flops 5242880 | bytes 20971520 | tf_op jit(solution)/shard_map/jit(_where)/select_n | solution.py:8
  39.5 0.7 all-gather.5.cloned.1.call-update
  40.2 0.7 all-gather.7.cloned.1.call-update
  40.9 0.5 all-gather.9.cloned.1.call-update
  41.5 15.5 %all-gather.11.cloned.1.call-done = bf16[256,2560]{1,0:T(8,128)(2,1)} async-done(((bf16[256,640]{1,0:T(8,128)(2,1)}), bf16[256,2560]{1,0:T(8,128)(2,1)}) %all-gather.11.cloned.1.call-update) | async-done | bytes 1310736 | tf_op jit(solution)/shard_map/all_gather | solution.py:71
  57.1 1.4 fusion.41
  58.5 3.7 fusion.4
  62.1 3.7 fusion.12
  65.9 0.9 fusion.6
  66.7 217.1 %all-reduce.3.cloned.1.call-done = (bf16[1024,2560]{1,0:T(8,128)(2,1)}, bf16[2560,1024]{1,0:T(8,128)(2,1)}, bf16[2560,1024]{1,0:T(8,128)(2,1)}) async-done(((bf16[1024,2560]{1,0:T(8,128)(2,1)}, bf16[2560,1024]{1,0:T(8,128)(2,1)}, bf16[2560,1024]{1,0:T(8,128)(2,1)}), (bf16[1024,2560]{1,0:T(8,128)(2,1)}, bf16[2560,1024]{1,0:T(8,128)(2,1)}, bf16[2560,1024]{1,0:T(8,128)(2,1)})) %all-reduce.3.cloned.1.call-update) | async-done | bytes 15728656 | tf_op jit(solution)/shard_map/psum | solution.py:9
  283.9 4.1 %fusion.43 = f32[128,1024]{1,0:T(8,128)} fusion(bf16[128,2560]{1,0:T(8,128)(2,1)S(1)} %bitcast.58, bf16[2560,1024]{1,0:T(8,128)(2,1)} %get-tuple-element.7), kind=kOutput, calls=%fused_computation.58 | convolution fusion | flops 671088640 | bytes 6422528 | tf_op jit(solution)/shard_map/dot_general | solution.py:13
  288.0 5.8 %fusion.21 = f32[128,2560]{1,0:T(8,128)S(1)} fusion(bf16[1024,2560]{1,0:T(8,128)(2,1)} %get-tuple-element.5, bf16[128,2560]{1,0:T(8,128)(2,1)S(1)} %bitcast.59, bf16[2560,1024]{1,0:T(8,128)(2,1)} %get-tuple-element.6, f32[128,1024]{1,0:T(8,128)} %fusion.43), kind=kOutput, calls=%fused_computation.24 | convolution fusion | flops 1342963712 | bytes 12976128 | tf_op jit(solution)/shard_map/dot_general | solution.py:16
  293.8 0.2 pad_maximum_fusion
  294.0 1.7 copy.12
  295.8 24.9 %all_gather.15 = bf16[128,2560]{1,0:T(8,128)(2,1)S(1)} all-gather(bf16[128,640]{1,0:T(8,128)(2,1)S(1)} %copy-done.2), channel_id=1, replica_groups=mesh['expert'=8,'tensor'=4] {'tensor'}, dimensions={1}, use_global_device_ids=true | all-gather | bytes 819200 | tf_op jit(solution)/shard_map/all_gather | solution.py:33
  320.7 3.4 fusion.42
  324.1 7.8 %fusion.22 = f32[128,2560]{1,0:T(8,128)} fusion(bf16[1024,2560]{0,1:T(8,128)(2,1)} %all-gather.9.cloned.1.call-done, bf16[128,2560]{1,0:T(8,128)(2,1)S(1)} %all_gather.15, bf16[2560,1024]{1,0:T(8,128)(2,1)} %all-gather.7.cloned.1.call-done, f32[128,1024]{1,0:T(8,128)S(1)} %fusion.42), kind=kOutput, calls=%fused_computation.25 | convolution fusion | flops 1342963712 | bytes 12976128 | tf_op jit(solution)/shard_map/dot_general | solution.py:55
  331.9 22.1 %reduce-scatter.5.cloned.1.call-done = f32[256,640]{1,0:T(8,128)} async-done(((f32[256,2560]{1,0:T(8,128)}), f32[256,640]{1,0:T(8,128)}) %reduce-scatter.5.cloned.1.call-update) | async-done | bytes 655376 | tf_op jit(solution)/shard_map/reduce_scatter | solution.py:90
  354.0 1.8 convert_element_type.31
  355.8 3.5 all-to-all-start.1
  359.3 0.3 fusion.20
  359.6 28.9 %reduce-scatter.3.cloned.1.call-done = f32[128,640]{1,0:T(8,128)} async-done(((f32[128,2560]{1,0:T(8,128)}), f32[128,640]{1,0:T(8,128)}) %reduce-scatter.3.cloned.1.call-update) | async-done | bytes 327696 | tf_op jit(solution)/shard_map/reduce_scatter | solution.py:60
  388.5 1.9 fusion.19
  (32 shorter events, 0.4 us)
Async XLA Ops:
  7.4 351.9 %copy-start = (bf16[2560,8]{0,1:T(8,128)(2,1)S(1)}, bf16[2560,8]{0,1:T(8,128)(2,1)}, u32[]{:S(2)}) copy-start(bf16[2560,8]{0,1:T(8,128)(2,1)} %param.15) | copy-start | bytes 122884
  11.7 12.8 %all-to-all-start = ((bf16[8,32,640]{2,1,0:T(8,128)(2,1)}), bf16[8,32,640]{2,1,0:T(8,128)(2,1)S(1)}, u32[]{:S(2)}, u32[]{:S(2)}) async-start(bf16[8,32,640]{2,1,0:T(8,128)(2,1)} %bitcast.3), calls=%async_computation.1 | async-start | bytes 655360 | tf_op jit(solution)/shard_map/all_to_all | solution.py:70
  16.9 40.2 %all-gather.11.cloned.1.call-start = ((), (), s32[]{:S(2)}) async-start(), calls=%async_computation.8 | async-start | bytes 1638400 | tf_op jit(solution)/shard_map/all_gather | solution.py:71
  24.5 0.7 copy-start.1
  25.2 258.6 %all-reduce.3.cloned.1.call-start = ((), (), s32[]{:S(2)}) async-start(), calls=%async_computation.10 | async-start | bytes 31457280 | tf_op jit(solution)/shard_map/psum | solution.py:9
  39.4 281.2 %all-gather.5.cloned.1.call-start = ((), (), s32[]{:S(2)}) async-start(), calls=%async_computation.4 | async-start | bytes 5898240 | tf_op jit(solution)/shard_map/all_gather | solution.py:46
  40.2 283.9 %all-gather.7.cloned.1.call-start = ((), (), s32[]{:S(2)}) async-start(), calls=%async_computation.5 | async-start | bytes 5898240 | tf_op jit(solution)/shard_map/all_gather | solution.py:51
  40.9 283.2 %all-gather.9.cloned.1.call-start = ((), (), s32[]{:S(2)}) async-start(), calls=%async_computation.6 | async-start | bytes 5898240 | tf_op jit(solution)/shard_map/all_gather | solution.py:57
  41.5 312.5 %reduce-scatter.5.cloned.1.call-start = ((), (), s32[]{:S(2)}) async-start(), calls=%async_computation.9 | async-start | bytes 3276800 | tf_op jit(solution)/shard_map/reduce_scatter | solution.py:90
  58.4 7.4 %slice-start = ((s8[5242880]{0:T(1024)(128)(4,1)}), s8[4194304]{0:T(1024)(128)(4,1)S(1)}, s32[]{:S(2)}) async-start(s8[5242880]{0:T(1024)(128)(4,1)} %bitcast.55), calls=%async_computation.11 | async-start | bytes 8388608
  62.1 3.7 slice-start.1
  294.0 1.8 copy-start.2
  295.7 92.8 %reduce-scatter.3.cloned.1.call-start = ((), (), s32[]{:S(2)}) async-start(), calls=%async_computation.7 | async-start | bytes 1638400 | tf_op jit(solution)/shard_map/reduce_scatter | solution.py:60
  324.0 7.9 %copy-start.3 = (s32[128,1]{0,1:T(1,128)S(1)}, s32[128,1]{0,1:T(1,128)}, u32[]{:S(2)}) copy-start(s32[128,1]{0,1:T(1,128)} %param.12) | copy-start | bytes 1540
  324.0 35.5 %copy-start.4 = (s32[128]{0:T(128)S(1)}, s32[128]{0:T(128)}, u32[]{:S(2)}) copy-start(s32[128]{0:T(128)} %param.13) | copy-start | bytes 1540
  355.8 32.7 %all-to-all-start.1 = ((bf16[8,32,640]{2,1,0:T(8,128)(2,1)}), bf16[8,32,640]{2,1,0:T(8,128)(2,1)S(1)}, u32[]{:S(2)}, u32[]{:S(2)}) async-start(bf16[8,32,640]{2,1,0:T(8,128)(2,1)} %bitcast.16), calls=%async_computation.3 | async-start | bytes 655360 | tf_op jit(solution)/shard_map/all_to_all | solution.py:93
Sparse Core Ops, SparseCore 0:
  25.4 31.6 all-gather.10
  58.9 54.3 all-gather.4
  115.2 62.2 all-gather.6
  179.2 57.2 all-gather.8
  295.9 58.0 reduce-scatter.4
  356.1 32.3 reduce-scatter.2
Sparse Core Ops, SparseCore 1:
  39.5 244.3 all-reduce.2
where the time goes:
time: 398 us
  waiting for transfers between devices  293 us (74%)
  matrix products  33.4 us (8%)
  blocking collectives  24.9 us (6%)
  other arithmetic  18.6 us (5%)
  between operations  15.8 us (4%)
  starting transfers between devices  8.93 us (2%)
    psum x1, waiting for transfers between devices, from_root(): return lax.psum(block, axis)  217 us
    reduce_scatter x1, waiting for transfers between devices, local(): lax.psum_scatter(shared_terms, 'tensor', scatter_dimension=1, tiled=True)  28.9 us
    all_gather x1, blocking collectives, local(): whole = lax.all_gather(tokens, 'tensor', axis=1, tiled=True)  24.9 us
    reduce_scatter x1, waiting for transfers between devices, local(): lax.psum_scatter(partials, 'tensor', scatter_dimension=1, tiled=True)  22.1 us
    all_gather x1, waiting for transfers between devices, local(): arrived = lax.all_gather(quarter, 'tensor', axis=1, tiled=True)  15.5 us
    select_n x2, other arithmetic, from_root(): jnp.where(lax.axis_index(axis) == source, block, jnp.zeros_like(block))  14.1 us
  transfers between devices with their start and end apart: 9, of which 5 were waited for; matrix products, arithmetic and copies ran while one was open for 12% of the time, Pallas kernels for 0%

commit v1 on v0

--- a/solution.py
+++ b/solution.py
@@ -6,7 +6,12 @@
 
 def from_root(block, axis, source):
     block = jnp.where(lax.axis_index(axis) == source, block, jnp.zeros_like(block))
-    return lax.psum(block, axis)
+
+    def build_strings(matrix):
+        before = lax.all_gather(matrix, axis_name=axis)
+        return jnp.sum(before, axis=0)
+
+    return build_strings(block)
 
 
 def expert_ffn(batch_rows, w_gate, w_up, w_down):

time: 398 us -> 876 us (2.20)
  waiting for transfers between devices: 293 us -> 724 us
  other arithmetic: 18.6 us -> 72.3 us
    all_gather x0 -> x3, waiting for transfers between devices: none -> 547 us  [build_strings(): before = lax.all_gather(matrix, axis_name=axis)]
    psum x1 -> x0, waiting for transfers between devices: 217 us -> none  [from_root(): return lax.psum(block, axis)]
    reduce_sum x0 -> x3, other arithmetic: none -> 59.8 us  [build_strings(): return jnp.sum(before, axis=0)]
    all_gather x1, waiting for transfers between devices: 0.02 us -> 42.9 us  [local(): lax.all_gather(sh_down, 'expert', axis=1, tiled=True)]
    all_gather x1, waiting for transfers between devices: 0.02 us -> 37 us  [local(): lax.all_gather(sh_up, 'expert', axis=0, tiled=True)]
    reduce_scatter x1, waiting for transfers between devices: 22.1 us -> 46.8 us  [local(): lax.psum_scatter(partials, 'tensor', scatter_dimension=1, tiled=True)]
    all_to_all x0 -> x1, blocking collectives: none -> 12.7 us  [local(): lax.all_to_all(outgoing, 'expert', split_axis=0, concat_axis=0, tiled=True)]
  transfers between devices with their start and end apart: 9 -> 10, of which waited for: 5 -> 8; matrix products, arithmetic and copies ran while one was open for 12% -> 11% of each run, Pallas kernels for 0% -> 0%
where the time goes in v1:
time: 876 us; the launch traced here: 875 us
  waiting for transfers between devices  724 us (83%)
  other arithmetic  72.3 us (8%)
  blocking collectives  31.1 us (4%)
  matrix products  25.2 us (3%)
  between operations  14.1 us (2%)
    all_gather x3, waiting for transfers between devices, build_strings(): before = lax.all_gather(matrix, axis_name=axis)  547 us
    reduce_sum x3, other arithmetic, build_strings(): return jnp.sum(before, axis=0)  59.8 us
    reduce_scatter x1, waiting for transfers between devices, local(): lax.psum_scatter(partials, 'tensor', scatter_dimension=1, tiled=True)  46.8 us
    all_gather x1, waiting for transfers between devices, local(): lax.all_gather(sh_down, 'expert', axis=1, tiled=True)  42.9 us
    all_gather x1, waiting for transfers between devices, local(): lax.all_gather(sh_up, 'expert', axis=0, tiled=True)  37 us
    reduce_scatter x1, waiting for transfers between devices, local(): lax.psum_scatter(shared_terms, 'tensor', scatter_dimension=1, tiled=True)  27.5 us
    all_gather x1, waiting for transfers between devices, local(): arrived = lax.all_gather(quarter, 'tensor', axis=1, tiled=True)  21 us
    all_gather x1, blocking collectives, local(): whole = lax.all_gather(tokens, 'tensor', axis=1, tiled=True)  18.3 us
  transfers between devices with their start and end apart: 10, of which 8 were waited for; matrix products, arithmetic and copies ran while one was open for 11% of the time, Pallas kernels for 0%

profile of v1, /device:TPU:0, one launch (start us, length us, event | category | flops | bytes accessed | tf_op | source)
XLA Modules:
  0.0 875.4 jit_solution(442983896324345497)
XLA Ops:
  6.5 0.7 fusion.35
  7.5 0.8 select_reduce_fusion
  9.0 1.1 convolution_convert_fusion
  10.1 12.7 %all_to_all.24 = bf16[8,32,640]{2,1,0:T(8,128)(2,1)} all-to-all(bf16[8,32,640]{2,1,0:T(8,128)(2,1)S(1)} %bitcast.73), channel_id=1, replica_groups=mesh['expert'=8,'tensor'=4] {'expert'}, dimensions={0} | all-to-all | bytes 655360 | tf_op jit(solution)/shard_map/all_to_all | solution.py:75
  23.6 2.7 broadcast_select_fusion.2
  26.3 2.6 broadcast_select_fusion.1
  29.0 2.6 broadcast_select_fusion
  33.6 21.0 %all-gather.14.cloned.1.call-done = bf16[256,2560]{1,0:T(8,128)(2,1)} async-done(((bf16[256,640]{1,0:T(8,128)(2,1)}), bf16[256,2560]{1,0:T(8,128)(2,1)}) %all-gather.14.cloned.1.call-update) | async-done | bytes 1310736 | tf_op jit(solution)/shard_map/all_gather | solution.py:76
  54.7 1.5 fusion.38
  56.2 3.6 fusion.6
  59.8 1.0 fusion.17
  61.2 0.9 fusion.8
  62.0 190.9 %all-gather.16.cloned.1.call-done = bf16[8,2560,1024]{2,1,0:T(8,128)(2,1)} async-done(((bf16[1,2560,1024]{2,1,0:T(8,128)(2,1)}), bf16[8,2560,1024]{2,1,0:T(8,128)(2,1)}) %all-gather.16.cloned.1.call-update) | async-done | bytes 41943056 | tf_op jit(solution)/shard_map/all_gather | solution.py:11
  252.9 20.8 %reduce_sum.56 = bf16[2560,1024]{1,0:T(8,128)(2,1)} reduce(bf16[8,2560,1024]{2,1,0:T(8,128)(2,1)} %all-gather.16.cloned.1.call-done, bf16[]{:T(256)} %constant.55.clone.1), dimensions={0}, to_apply=%region_4.5 | reduce | flops 18350080 | bytes 47185920 | tf_op jit(solution)/shard_map/reduce_sum | solution.py:12
  273.8 178.1 %all-gather.18.cloned.1.call-done = bf16[8,2560,1024]{2,1,0:T(8,128)(2,1)} async-done(((bf16[1,2560,1024]{2,1,0:T(8,128)(2,1)}), bf16[8,2560,1024]{2,1,0:T(8,128)(2,1)}) %all-gather.18.cloned.1.call-update) | async-done | bytes 41943056 | tf_op jit(solution)/shard_map/all_gather | solution.py:11
  451.9 20.9 %reduce_sum.57 = bf16[2560,1024]{1,0:T(8,128)(2,1)} reduce(bf16[8,2560,1024]{2,1,0:T(8,128)(2,1)} %all-gather.18.cloned.1.call-done, bf16[]{:T(256)} %constant.55.clone.1), dimensions={0}, to_apply=%region_5.6 | reduce | flops 18350080 | bytes 47185920 | tf_op jit(solution)/shard_map/reduce_sum | solution.py:12
  472.8 177.9 %all-gather.20.cloned.1.call-done = bf16[8,1024,2560]{2,1,0:T(8,128)(2,1)} async-done(((bf16[1,1024,2560]{2,1,0:T(8,128)(2,1)}), bf16[8,1024,2560]{2,1,0:T(8,128)(2,1)}) %all-gather.20.cloned.1.call-update) | async-done | bytes 41943056 | tf_op jit(solution)/shard_map/all_gather | solution.py:11
  650.7 18.1 %reduce_sum.58 = bf16[1024,2560]{1,0:T(8,128)(2,1)} reduce(bf16[8,1024,2560]{2,1,0:T(8,128)(2,1)} %all-gather.20.cloned.1.call-done, bf16[]{:T(256)} %constant.55.clone.1), dimensions={0}, to_apply=%region_6.7 | reduce | flops 18350080 | bytes 47185920 | tf_op jit(solution)/shard_map/reduce_sum | solution.py:12
  668.7 3.5 fusion.40
  672.8 1.0 fusion.21
  674.6 0.9 fusion.11
  675.7 1.7 copy.13
  677.4 18.3 %all_gather.27 = bf16[128,2560]{1,0:T(8,128)(2,1)S(1)} all-gather(bf16[128,640]{1,0:T(8,128)(2,1)S(1)} %copy-done.2), channel_id=1, replica_groups=mesh['expert'=8,'tensor'=4] {'tensor'}, dimensions={1}, use_global_device_ids=true | all-gather | bytes 819200 | tf_op jit(solution)/shard_map/all_gather | solution.py:38
  695.8 3.3 fusion.39
  699.2 37.0 %all-gather.10.cloned.1.call-done = bf16[2560,1024]{1,0:T(8,128)(2,1)} async-done(((bf16[320,1024]{1,0:T(8,128)(2,1)}), bf16[2560,1024]{1,0:T(8,128)(2,1)}) %all-gather.10.cloned.1.call-update) | async-done | bytes 5242896 | tf_op jit(solution)/shard_map/all_gather | solution.py:56
  736.2 42.9 %all-gather.12.cloned.1.call-done = bf16[1024,2560]{0,1:T(8,128)(2,1)} async-done(((bf16[1024,320]{0,1:T(8,128)(2,1)}), bf16[1024,2560]{0,1:T(8,128)(2,1)}) %all-gather.12.cloned.1.call-update) | async-done | bytes 5242896 | tf_op jit(solution)/shard_map/all_gather | solution.py:62
  779.1 7.8 fusion.26
  786.9 46.8 %reduce-scatter.5.cloned.1.call-done = f32[256,640]{1,0:T(8,128)} async-done(((f32[256,2560]{1,0:T(8,128)}), f32[256,640]{1,0:T(8,128)}) %reduce-scatter.5.cloned.1.call-update) | async-done | bytes 655376 | tf_op jit(solution)/shard_map/reduce_scatter | solution.py:95
  833.7 1.8 convert_element_type.37
  835.5 3.7 all-to-all-start.1
  839.5 27.5 %reduce-scatter.3.cloned.1.call-done = f32[128,640]{1,0:T(8,128)} async-done(((f32[128,2560]{1,0:T(8,128)}), f32[128,640]{1,0:T(8,128)}) %reduce-scatter.3.cloned.1.call-update) | async-done | bytes 327696 | tf_op jit(solution)/shard_map/reduce_scatter | solution.py:65
  866.9 1.9 fusion.24
  (52 shorter events, 5.2 us)
Async XLA Ops:
  6.5 832.6 %copy-start = (bf16[2560,8]{0,1:T(8,128)(2,1)S(1)}, bf16[2560,8]{0,1:T(8,128)(2,1)}, u32[]{:S(2)}) copy-start(bf16[2560,8]{0,1:T(8,128)(2,1)} %param.15) | copy-start | bytes 122884
  6.5 48.1 %all-gather.14.cloned.1.call-start = ((), (), s32[]{:S(2)}) async-start(), calls=%async_computation.8 | async-start | bytes 1638400 | tf_op jit(solution)/shard_map/all_gather | solution.py:76
  22.9 230.1 %all-gather.16.cloned.1.call-start = ((), (), s32[]{:S(2)}) async-start(), calls=%async_computation.9 | async-start | bytes 47185920 | tf_op jit(solution)/shard_map/all_gather | solution.py:11
  26.3 425.6 %all-gather.18.cloned.1.call-start = ((), (), s32[]{:S(2)}) async-start(), calls=%async_computation.10 | async-start | bytes 47185920 | tf_op jit(solution)/shard_map/all_gather | solution.py:11
  29.0 621.7 %all-gather.20.cloned.1.call-start = ((), (), s32[]{:S(2)}) async-start(), calls=%async_computation.11 | async-start | bytes 47185920 | tf_op jit(solution)/shard_map/all_gather | solution.py:11
  31.6 28.1 %slice-start.4 = ((s8[5242880]{0:T(1024)(128)(4,1)}), s8[1048576]{0:T(1024)(128)(4,1)S(1)}, s32[]{:S(2)}) async-start(s8[5242880]{0:T(1024)(128)(4,1)} %bitcast.64), calls=%async_computation.17 | async-start | bytes 2097152
  31.7 664.1 %all-gather.8.cloned.1.call-start = ((), (), s32[]{:S(2)}) async-start(), calls=%async_computation.4 | async-start | bytes 5898240 | tf_op jit(solution)/shard_map/all_gather | solution.py:51
  32.3 703.9 %all-gather.10.cloned.1.call-start = ((), (), s32[]{:S(2)}) async-start(), calls=%async_computation.5 | async-start | bytes 5898240 | tf_op jit(solution)/shard_map/all_gather | solution.py:56
  32.8 746.2 %all-gather.12.cloned.1.call-start = ((), (), s32[]{:S(2)}) async-start(), calls=%async_computation.6 | async-start | bytes 5898240 | tf_op jit(solution)/shard_map/all_gather | solution.py:62
  33.6 800.1 %reduce-scatter.5.cloned.1.call-start = ((), (), s32[]{:S(2)}) async-start(), calls=%async_computation.12 | async-start | bytes 3276800 | tf_op jit(solution)/shard_map/reduce_scatter | solution.py:95
  54.7 5.1 slice-start.5
  56.2 4.6 slice-start.2
  59.8 1.4 slice-start.3
  668.7 4.0 copy-start.1
  668.7 5.3 slice-start
  672.8 1.8 slice-start.1
  675.7 1.8 copy-start.2
  677.4 189.6 %reduce-scatter.3.cloned.1.call-start = ((), (), s32[]{:S(2)}) async-start(), calls=%async_computation.7 | async-start | bytes 1638400 | tf_op jit(solution)/shard_map/reduce_scatter | solution.py:65
  699.1 87.7 %copy-start.3 = (s32[128,1]{0,1:T(1,128)S(1)}, s32[128,1]{0,1:T(1,128)}, u32[]{:S(2)}) copy-start(s32[128,1]{0,1:T(1,128)} %param.12) | copy-start | bytes 1540
  699.1 140.3 %copy-start.4 = (s32[128]{0:T(128)S(1)}, s32[128]{0:T(128)}, u32[]{:S(2)}) copy-start(s32[128]{0:T(128)} %param.13) | copy-start | bytes 1540
  835.5 31.4 %all-to-all-start.1 = ((bf16[8,32,640]{2,1,0:T(8,128)(2,1)}), bf16[8,32,640]{2,1,0:T(8,128)(2,1)S(1)}, u32[]{:S(2)}, u32[]{:S(2)}) async-start(bf16[8,32,640]{2,1,0:T(8,128)(2,1)} %bitcast.18), calls=%async_computation.3 | async-start | bytes 655360 | tf_op jit(solution)/shard_map/all_to_all | solution.py:98
Sparse Core Ops, SparseCore 0:
  23.0 31.6 all-gather.13
  56.6 196.2 all-gather.15
  254.8 196.9 all-gather.17
  453.6 196.9 all-gather.19
  652.4 40.9 all-gather.7
  695.2 40.9 all-gather.9
  738.1 40.9 all-gather.11
  781.4 52.2 reduce-scatter.4
  836.0 30.9 reduce-scatter.2
